TPU v7x, 128 devices: a whole 4x4x4 slice. The times are simulated.
128 devices in a mesh: dev: 128 (over x, z, y, core).
Axes of the slice: x: 4, y: 4, z: 4, core: 2. Of those that a mesh axis runs over, the one named last changes fastest.
Arguments:
- pixels: bfloat16 [128, 256, 16], P('dev'), may hold values from -6 to 6
- embed_w: bfloat16 [128, 16, 8192], P('dev'), may hold values from -1.5 to 1.5
- var_embed: bfloat16 [128, 8192], P('dev'), may hold values from -3 to 3
- key_w: bfloat16 [8192, 8192], P('dev'), may hold values from -0.0625 to 0.0625
- query: float32 [8192], replicated, may hold values from -500 to 500
- value_t: bfloat16 [8192, 8192], P('dev'), may hold values from -0.0625 to 0.0625
- out_w: bfloat16 [8192, 8192], P('dev'), may hold values from -0.0625 to 0.0625
Outputs:
- mixed: bfloat16 [256, 8192], P('dev')
All inputs are finite; a program needn't handle non-finite values.
Results may differ from a plain program's by a relative error of at most 0.012.
The roundings to bfloat16 on the way count: a program that leaves them out, or rounds other values in their place, can miss the bound.
Values may be sent and summed in bfloat16 or wider, within the bound.
A program may use at most 64 MiB of HBM per device.

v0:
```python
import jax
import jax.numpy as jnp
from jax import lax
from jax.sharding import PartitionSpec as P

D = 8192
HEADS = 64
HD = 128
V = 91


def body(pixels, embed_w, var_embed, key_w, query, value_t, out_w):
    group_size = lax.axis_size("dev")
    own_embed = jnp.einsum("vtp,vpd->vtd", pixels, embed_w, preferred_element_type=jnp.float32)
    own_embed = (own_embed + var_embed.astype(jnp.float32)[:, None, :]).astype(jnp.bfloat16)
    grouped = lax.all_to_all(own_embed, "dev", split_axis=1, concat_axis=0, tiled=True)
    key_rows = key_w.shape[0]
    keyq_part = jnp.einsum(
        "dhj,hj->dh",
        key_w.astype(jnp.float32).reshape(key_rows, HEADS, HD),
        query.reshape(HEADS, HD),
        precision=lax.Precision.HIGHEST,
    )
    keyq = lax.all_gather(keyq_part, "dev", axis=0, tiled=True)
    logits = jnp.einsum(
        "vtd,dh->vth", grouped.astype(jnp.float32), keyq, precision=lax.Precision.HIGHEST
    ) / jnp.sqrt(jnp.float32(HD))
    slot = lax.broadcasted_iota(jnp.int32, logits.shape, 0)
    logits = jnp.where(slot < V, logits, -1e30)
    row_max = jnp.max(logits, axis=0, keepdims=True)
    weights = jnp.exp(logits - row_max)
    attn = (weights / jnp.sum(weights, axis=0, keepdims=True)).astype(jnp.bfloat16)
    pooled = jnp.einsum("vth,vtd->thd", attn, grouped, preferred_element_type=jnp.float32).astype(
        jnp.bfloat16
    )
    spread = jnp.repeat(pooled, group_size // HEADS, axis=1)[:, :, None, :]
    received = lax.all_to_all(spread, "dev", split_axis=1, concat_axis=0, tiled=True)
    all_tokens = received.shape[0]
    head_share = received.shape[2]
    received = received.reshape(all_tokens, head_share, D)
    columns = value_t.shape[0]
    value_heads = jnp.einsum(
        "thd,hcd->thc",
        received,
        value_t.reshape(head_share, columns // head_share, D),
        preferred_element_type=jnp.float32,
    )
    value_heads = value_heads.reshape(all_tokens, columns).astype(jnp.bfloat16)
    weight_cols = lax.all_to_all(out_w, "dev", split_axis=1, concat_axis=0, tiled=True)
    outcols = jnp.dot(
        lax.all_gather(value_heads, "dev", axis=1, tiled=True),
        weight_cols,
        preferred_element_type=jnp.float32,
    )
    return lax.all_to_all(
        outcols.astype(jnp.bfloat16), "dev", split_axis=0, concat_axis=1, tiled=True
    )


def solution(mesh):
    placed = (
        P("dev", None, None),
        P("dev", None, None),
        P("dev", None),
        P("dev", None),
        P(),
        P("dev", None),
        P("dev", None),
    )
    return jax.shard_map(
        body, mesh=mesh, in_specs=placed, out_specs=P("dev", None), check_vma=False
    )
```

profile of v0, /device:TPU:1, one launch (start us, length us, event | category | flops | bytes accessed | tf_op | source)
XLA Modules:
  0.0 380.6 jit_solution(134359456119884214)
XLA Ops:
  6.5 0.0 copy-start
  6.5 0.9 add.17
  7.4 2.2 fusion.2
  9.7 20.2 %copy.55 = bf16[1,256,8192]{2,0,1:T(2,128)(2,1)} copy(bf16[1,256,8192]{2,1,0:T(8,128)(2,1)S(1)} %fusion.2) | data formatting | bytes 8388608 | tf_op jit(solution)/shard_map/convert_element_type | solution.py:15
  29.9 0.5 broadcast.8
  30.4 26.9 %reduce.2 = bf16[256,8192]{1,0:T(8,128)(2,1)} reduce(bf16[256,1,8192]{2,1,0:T(2,128)(2,1)} %bitcast.58, bf16[]{:T(256)} %broadcast.8), dimensions={1}, to_apply=%bitcast.56.reduce_sub_computation | reduce | bytes 8388610
  57.3 7.6 %reshape.53 = bf16[128,2,8192]{2,1,0:T(2,128)(2,1)} reshape(bf16[256,8192]{1,0:T(8,128)(2,1)} %reduce.2) | data formatting | bytes 8388608
  64.9 0.0 copy-start.2
  64.9 0.0 copy-start.3
  64.9 11.9 %all-to-all-start = ((bf16[128,2,8192]{2,1,0:T(2,128)(2,1)}), bf16[128,2,8192]{2,1,0:T(2,128)(2,1)}, u32[]{:S(2)}, u32[]{:S(2)}) async-start(bf16[128,2,8192]{2,1,0:T(2,128)(2,1)} %reshape.53), calls=%async_computation | async-start | bytes 8388608 | tf_op jit(solution)/shard_map/all_to_all | solution.py:16
  76.8 0.0 all-gather.3.cloned.1.call-start
  76.9 0.0 copy-done.2
  76.9 0.0 copy-done.3
  76.9 1.7 fusion.19
  78.6 0.7 copy.35
  79.3 0.0 all-gather.3.cloned.1.call-update
  79.4 0.0 all-gather.5.cloned.1.call-start
  79.4 50.3 %all-to-all-done = bf16[128,2,8192]{2,1,0:T(2,128)(2,1)} async-done(((bf16[128,2,8192]{2,1,0:T(2,128)(2,1)}), bf16[128,2,8192]{2,1,0:T(2,128)(2,1)}, u32[]{:S(2)}, u32[]{:S(2)}) %all-to-all-start) | async-done | bytes 4194336 | tf_op jit(solution)/shard_map/all_to_all | solution.py:16
  129.7 19.8 %reshape.54 = bf16[256,1,8192]{2,1,0:T(2,128)(2,1)} reshape(bf16[128,2,8192]{2,1,0:T(2,128)(2,1)} %all-to-all-done) | data formatting | bytes 8388608
  149.5 27.7 %bitcast_reduce_fusion = bf16[256,8192]{1,0:T(8,128)(2,1)} fusion(bf16[256,1,8192]{2,1,0:T(2,128)(2,1)} %reshape.54), kind=kLoop, calls=%fused_computation.25 | loop fusion | bytes 8388608 | tf_op jit(solution)/shard_map/all_to_all | solution.py:16
  177.2 7.6 %all_to_all.49 = bf16[128,2,8192]{2,1,0:T(2,128)(2,1)} reshape(bf16[256,8192]{1,0:T(8,128)(2,1)} %bitcast_reduce_fusion) | data formatting | bytes 8388608 | tf_op jit(solution)/shard_map/all_to_all | solution.py:16
  184.8 0.0 all-gather.3.cloned.1.call-done
  184.8 11.0 %fusion.14 = f32[128,2,64]{0,2,1:T(8,128)S(1)} fusion(f32[8192,64]{1,0:T(8,128)} %all-gather.3.cloned.1.call-done, bf16[128,2,8192]{2,1,0:T(2,128)(2,1)} %all_to_all.49, pred[128]{0:T(512)(128)(4,1)S(1)} %iota_compare_fusion), kind=kOutput, calls=%fused_computation.14 | convolution fusion | flops 1610645504 | bytes 6357120 | tf_op jit(solution)/shard_map/vtd,dh->vth/dot_general | solution.py:25
  195.8 0.2 fusion.26
  196.0 8.7 %convolution_convert_fusion = bf16[2,64,8192]{2,1,0:T(8,128)(2,1)} fusion(bf16[128,2,8192]{2,1,0:T(2,128)(2,1)} %all_to_all.49, f32[2,64]{1,0:T(2,128)S(1)} %fusion.26, f32[128,2,64]{0,2,1:T(8,128)S(1)} %fusion.14), kind=kOutput, calls=%fused_computation.4 | convolution fusion | flops 269533440 | bytes 6357504 | tf_op jit(solution)/shard_map/vth,vtd->thd/dot_general | solution.py:33
  204.7 3.8 copy.28
  208.5 6.2 %broadcast_in_dim.11 = bf16[2,64,2,8192]{3,0,2,1:T(2,128)(2,1)} broadcast(bf16[2,64,8192]{2,0,1:T(2,128)(2,1)S(1)} %copy.28), dimensions={0,1,3} | broadcast | bytes 6291456 | tf_op jit(solution)/shard_map/broadcast_in_dim | solution.py:36
  214.7 58.7 %all_to_all.65 = bf16[2,128,1,8192]{3,0,2,1:T(2,128)(2,1)} all-to-all(bf16[2,128,1,8192]{3,0,2,1:T(2,128)(2,1)} %bitcast.59), channel_id=1, replica_groups=mesh['dev'=128] {'dev'}, dimensions={1} | all-to-all | bytes 8388608 | tf_op jit(solution)/shard_map/all_to_all | solution.py:37
  273.3 7.2 %reshape.45 = bf16[256,8192]{1,0:T(8,128)(2,1)} reshape(bf16[128,2,1,1,8192]{4,1,0,3,2:T(2,128)(2,1)} %bitcast.60) | data formatting | bytes 8388608 | tf_op jit(solution)/shard_map/reshape.13
  280.5 0.0 copy-done
  280.5 0.0 copy-start.1
  280.5 4.3 %convolution_convert_fusion.1 = bf16[256,64]{0,1:T(8,128)(2,1)} fusion(bf16[256,8192]{1,0:T(8,128)(2,1)} %reshape.45, bf16[64,8192]{1,0:T(8,128)(2,1)S(1)} %copy-done), kind=kOutput, calls=%fused_computation.12 | convolution fusion | flops 268451840 | bytes 5275648 | tf_op jit(solution)/shard_map/thd,hcd->thc/dot_general | solution.py:42
  284.8 0.0 all-gather.5.cloned.1.call-update
  284.9 0.0 copy-done.1
  284.9 3.3 all_to_all.53
  288.2 2.9 copy.56
  291.1 2.3 reshape.51
  293.4 24.8 %all_to_all.66 = bf16[128,2,2048]{2,1,0:T(2,128)(2,1)} all-to-all(bf16[128,2,2048]{2,1,0:T(2,128)(2,1)} %reshape.51), channel_id=1, replica_groups=mesh['dev'=128] {'dev'}, dimensions={0} | all-to-all | bytes 2097152 | tf_op jit(solution)/shard_map/all_to_all | solution.py:49
  318.2 3.8 reshape.52
  322.0 32.9 %all-gather.5.cloned.1.call-done = bf16[256,8192]{0,1:T(8,128)(2,1)} async-done(((bf16[256,64]{0,1:T(8,128)(2,1)}), bf16[256,8192]{0,1:T(8,128)(2,1)}) %all-gather.5.cloned.1.call-update) | async-done | bytes 4194320 | tf_op jit(solution)/shard_map/all_gather | solution.py:51
  354.9 3.1 convolution_convert_fusion.2
  358.0 0.1 copy.31
  358.1 14.9 %all_to_all.67 = bf16[128,2,64]{2,1,0:T(2,128)(2,1)S(1)} all-to-all(bf16[128,2,64]{2,1,0:T(2,128)(2,1)S(1)} %bitcast.63), channel_id=1, replica_groups=mesh['dev'=128] {'dev'}, dimensions={0} | all-to-all | bytes 65536 | tf_op jit(solution)/shard_map/all_to_all | solution.py:55
  373.0 0.7 all_to_all.60
  (2 shorter events, 0.0 us)
Async XLA Ops:
  6.5 274.0 %copy-start = (bf16[64,8192]{1,0:T(8,128)(2,1)S(1)}, bf16[64,8192]{1,0:T(8,128)(2,1)}, u32[]{:S(2)}) copy-start(bf16[64,8192]{1,0:T(8,128)(2,1)} %param.12) | copy-start | bytes 3145732
  64.9 12.0 %copy-start.2 = (bf16[64,8192]{1,0:T(8,128)(2,1)S(1)}, bf16[64,8192]{1,0:T(8,128)(2,1)}, u32[]{:S(2)}) copy-start(bf16[64,8192]{1,0:T(8,128)(2,1)} %param.10) | copy-start | bytes 3145732
  64.9 12.0 %copy-start.3 = (f32[8192]{0:T(1024)S(1)}, f32[8192]{0:T(1024)}, u32[]{:S(2)}) copy-start(f32[8192]{0:T(1024)} %param.11) | copy-start | bytes 98308
  64.9 64.8 %all-to-all-start = ((bf16[128,2,8192]{2,1,0:T(2,128)(2,1)}), bf16[128,2,8192]{2,1,0:T(2,128)(2,1)}, u32[]{:S(2)}, u32[]{:S(2)}) async-start(bf16[128,2,8192]{2,1,0:T(2,128)(2,1)} %reshape.53), calls=%async_computation | async-start | bytes 8388608 | tf_op jit(solution)/shard_map/all_to_all | solution.py:16
  76.8 108.0 %all-gather.3.cloned.1.call-start = ((), (), s32[]{:S(2)}) async-start(), calls=%async_computation.4 | async-start | bytes 4227072 | tf_op jit(solution)/shard_map/all_gather | solution.py:24
  79.4 275.6 %all-gather.5.cloned.1.call-start = ((), (), s32[]{:S(2)}) async-start(), calls=%async_computation.5 | async-start | bytes 4227072 | tf_op jit(solution)/shard_map/all_gather | solution.py:51
  280.5 4.3 %copy-start.1 = (bf16[64,8192]{1,0:T(8,128)(2,1)S(1)}, bf16[64,8192]{1,0:T(8,128)(2,1)}, u32[]{:S(2)}) copy-start(bf16[64,8192]{1,0:T(8,128)(2,1)} %param.13) | copy-start | bytes 3145732
Sparse Core Ops, SparseCore 0:
  80.8 92.7 all-gather.2
  285.0 69.8 all-gather.4
where the time goes:
time: 382 us; the launch traced here: 381 us
  local copies, waits for them, and re-layouts  115 us (30%)
  blocking collectives  98.3 us (26%)
  waiting for transfers between devices  83.2 us (22%)
  matrix products  31.1 us (8%)
  other arithmetic  27.9 us (7%)
  between operations  13.5 us (4%)
  starting transfers between devices  12 us (3%)
    all_to_all x1, blocking collectives, body(): lax.all_to_all(spread, 'dev', split_axis=1, concat_axis=0, tiled=True)  58.7 us
    all_to_all x1, waiting for transfers between devices, body(): lax.all_to_all(own_embed, 'dev', split_axis=1, concat_axis=0, tiled=True)  50.3 us
    all_to_all x2, local copies, waits for them, and re-layouts, body(): lax.all_to_all(own_embed, 'dev', split_axis=1, concat_axis=0, tiled=True)  35.3 us
    unnamed x13, local copies, waits for them, and re-layouts  34 us
    all_gather x1, waiting for transfers between devices, body(): lax.all_gather(value_heads, 'dev', axis=1, tiled=True)  32.9 us
    unnamed x1, other arithmetic  26.9 us
    all_to_all x1, blocking collectives, body(): lax.all_to_all(out_w, 'dev', split_axis=1, concat_axis=0, tiled=True)  24.8 us
    convert_element_type x1, local copies, waits for them, and re-layouts, body(): (own_embed + var_embed.astype(jnp.float32)[:, None, :]).astype(jnp.bfloat16)  20.2 us
  transfers between devices with their start and end apart: 3, of which 2 were waited for; matrix products, arithmetic and copies ran while one was open for 15% of the time, Pallas kernels for 0%

commit v1 on v0

v1 whole, which is shorter than its diff:
```python
import jax
import jax.numpy as jnp
from jax import lax
from jax.experimental import pallas as pl
from jax.experimental.pallas import tpu as pltpu
from jax.sharding import PartitionSpec as P

D = 8192
HEADS = 64
HD = 128
V = 91
MESH = pl.DeviceIdType.MESH
BF = jnp.bfloat16
F32 = jnp.float32
OFFSETS = (0, -1, 1, 2)


def dot(a, b, dims):
    return lax.dot_general(a, b, (dims, ((), ())), preferred_element_type=F32)


def kernel(
    pix_ref,
    ew_ref,
    var_ref,
    kw_ref,
    q_ref,
    vt_ref,
    ow_ref,
    out_ref,
    kw,
    ew,
    vf,
    pixp,
    pixt,
    wpart,
    vpart,
    ppart,
    emb,
    kqs,
    kq,
    eb,
    vs,
    px,
    vt,
    ow,
    lps,
    lpr,
    ls,
    lq,
    lr,
    aw,
    evt,
    at,
    hp,
    hr,
    hg,
    ms,
    mr,
    ob,
    obr,
    loc_sem,
    ssem,
    el_rs,
    vl_rs,
    pl_rs,
    part_rs,
    kl_rs,
    vt_rs,
    ow_rs,
    kag_rs,
    eag_rs,
    pag_rs,
    lp_rs,
    lq_rs,
    lr_rs,
    hr_rs,
    hg_rs,
    mr_rs,
    ob_rs,
):
    me = lax.axis_index("dev")
    x = lax.div(me, 32)
    p = lax.rem(lax.div(me, 2), 16)
    c = lax.rem(me, 2)
    z = lax.div(p, 4)
    y = lax.rem(p, 4)
    s = 2 * x + c
    partner = x * 32 + p * 2 + (1 - c)
    source = x < 3

    def dev(s_, p_):
        return lax.div(s_, 2) * 32 + p_ * 2 + lax.rem(s_, 2)

    def wrap8(v):
        return lax.rem(v + 8, 8)

    def wrap16(v):
        return lax.rem(v + 16, 16)

    pending = []
    counter = [0]

    def send(src, dst, rs, d, like=None):
        number = counter[0]
        counter[0] += 1
        sem = ssem.at[number]
        pltpu.make_async_remote_copy(
            src_ref=src, dst_ref=dst, send_sem=sem, recv_sem=rs, device_id=(d,), device_id_type=MESH
        ).start()
        if like is None:
            pending.append((src, sem))
        return like, number

    def wait(ref, sem):
        pltpu.make_async_copy(ref, ref, sem).wait()

    def drain(pairs):
        for like, number in pairs:
            wait(like(), ssem.at[number])

    barrier = pltpu.get_barrier_semaphore()
    for k in range(1, 8):
        pl.semaphore_signal(barrier, inc=1, device_id=(dev(wrap8(s + k), p),), device_id_type=MESH)
    for k in range(1, 16):
        pl.semaphore_signal(barrier, inc=1, device_id=(dev(s, wrap16(p + k)),), device_id_type=MESH)
    kw_in = pltpu.make_async_copy(kw_ref, kw, loc_sem.at[0])
    kw_in.start()
    ew_in = pltpu.make_async_copy(ew_ref.at[0], ew, loc_sem.at[1])
    ew_in.start()

    pos = lax.broadcasted_iota(jnp.int32, (256, 256), 0)
    tok = lax.broadcasted_iota(jnp.int32, (256, 256), 1)
    want = lax.div(lax.rem(pos, 16), 4) * 64 + lax.div(pos, 16) * 4 + lax.rem(pos, 4)
    perm = jnp.where(tok == want, 1.0, 0.0).astype(BF)
    ordered = dot(perm, pix_ref[0], ((1,), (0,))).astype(BF)
    pixp[...] = ordered
    eye = jnp.where(
        lax.broadcasted_iota(jnp.int32, (16, 16), 0) == lax.broadcasted_iota(jnp.int32, (16, 16), 1), 1.0, 0.0
    ).astype(BF)
    pixt[...] = dot(eye, ordered, ((1,), (1,))).astype(BF)
    for k in range(8):
        vf[k] = var_ref[:, k * 1024 : (k + 1) * 1024].astype(F32)
    eb[:, 7] = jnp.zeros((16, 16, 1024), BF)
    ew_in.wait()
    pl.semaphore_wait(barrier, 22)

    half = pl.multiple_of((1 - c) * 4096, 4096)
    first_sends = []
    line_ids = [wrap8(s + k) for k in range(1, 8)]

    @pl.when(source)
    def _():
        first_sends.append(send(ew.at[:, pl.ds(half, 4096)], wpart, part_rs.at[0], partner, lambda: ew.at[:, 0:4096]))
        first_sends.append(send(vf.at[pl.ds(4 * (1 - c), 4)], vpart, part_rs.at[1], partner, lambda: vf.at[0:4]))
        first_sends.append(send(pixp, ppart, part_rs.at[2], partner, lambda: pixp))
        pltpu.make_async_copy(ew.at[:, pl.ds(pl.multiple_of(s * 1024, 1024), 1024)], eb.at[p, s], el_rs.at[s]).start()
        pltpu.make_async_copy(vf.at[s], vs.at[s], vl_rs.at[s]).start()
        pltpu.make_async_copy(pixt, px.at[p, s], pl_rs.at[s]).start()
        for sd in line_ids:
            col = pl.ds(pl.multiple_of(sd * 1024, 1024), 1024)
            first_sends.append(send(ew.at[:, col], eb.at[p, s], el_rs.at[s], dev(sd, p), lambda: ew.at[:, 0:1024]))
            first_sends.append(send(vf.at[sd], vs.at[s], vl_rs.at[s], dev(sd, p), lambda: vf.at[0]))
            first_sends.append(send(pixt, px.at[p, s], pl_rs.at[s], dev(sd, p), lambda: pixt))

    own_col = pl.ds(pl.multiple_of(s * 1024, 1024), 1024)
    pltpu.make_async_copy(vt_ref.at[:, own_col], vt.at[s], vt_rs.at[s]).start()
    for sd in line_ids:
        col = pl.ds(pl.multiple_of(sd * 1024, 1024), 1024)
        send(vt_ref.at[:, col], vt.at[s], vt_rs.at[s], dev(sd, p))

    kw_in.wait()
    lane = lax.broadcasted_iota(jnp.int32, (64, 128), 1)
    folded = jnp.where(lane < 64, lane, lane - 64)
    acc = jnp.zeros((64, 128), F32)
    for h in range(HEADS):
        cut = slice(h * HD, (h + 1) * HD)
        total = jnp.sum(kw[:, cut].astype(F32) * q_ref[:, cut], axis=1, keepdims=True)
        acc = jnp.where(folded == (h % 16) * 4 + h // 16, total, acc)
    high = acc.astype(BF).astype(F32)
    kqs[...] = jnp.where(lane < 64, high, acc - high).astype(BF)

    key_half = lax.rem(x, 2)
    key_core = lax.div(x, 2)
    key_sends = []
    for xd in range(3):
        target = dev(2 * xd + key_core, p)
        dst = kq.at[key_half, p, pl.ds(pl.multiple_of(c * 64, 64), 64), :]
        sem = kl_rs.at[key_half, c]

        away = target != me

        @pl.when(away)
        def _():
            key_sends.append((away, send(kqs, dst, sem, target, lambda: kqs)))

        @pl.when(target == me)
        def _():
            pltpu.make_async_copy(kqs, dst, sem).start()

    def place(oz, oy):
        return lax.rem(z + oz + 4, 4) * 4 + lax.rem(y + oy + 4, 4)

    def spread(dist, half_id, payloads, conditional=None):
        for o1 in OFFSETS:
            for o2 in OFFSETS:
                if abs(o1) + abs(o2) != dist:
                    continue
                oy, oz = (o1, o2) if half_id == 0 else (o2, o1)
                item = place(oz, oy)
                if dist > 0:
                    for ref_of, sems in payloads:
                        wait(ref_of(half_id, item), sems.at[half_id, item])
                sign = 1 if half_id == 0 else -1
                moves = []
                if o2 == 0:
                    if o1 == 0:
                        moves += [(1, 0), (-1, 0)]
                    elif o1 == -sign:
                        moves += [(sign, 0)]
                    moves += [(0, 1), (0, -1)]
                else:
                    f2 = sign if o1 in (0, 2) else -sign
                    if o2 == -f2:
                        moves += [(0, f2)]
                for m1, m2 in moves:
                    my, mz = (m1, m2) if half_id == 0 else (m2, m1)
                    target = dev(s, place(mz, my))
                    for ref_of, sems in payloads:
                        ref = ref_of(half_id, item)
                        if conditional is None:
                            send(ref, ref, sems.at[half_id, item], target)
                        else:
                            conditional.append(send(ref, ref, sems.at[half_id, item], target, lambda: ref_of(0, 0)))

    def key_block(half_id, item):
        return kq.at[half_id, item]

    def embed_block(half_id, item):
        return eb.at[item, pl.ds(0, 7), :, pl.ds(half_id * 512, 512)]

    def pixel_block(half_id, item):
        return px.at[item, :, :, pl.ds(half_id * 128, 128)]

    e_payloads = ((embed_block, eag_rs), (pixel_block, pag_rs))
    k_payloads = ((key_block, kag_rs),)
    k_sends = []

    def spread_keys(dist):
        @pl.when(source)
        def _():
            for half_id in (0, 1):
                spread(dist, half_id, k_payloads, k_sends)

    def spread_embed(dist):
        for half_id in (0, 1):
            spread(dist, half_id, e_payloads)

    @pl.when(source)
    def _():
        for a in range(2):
            for b in range(2):
                wait(kq.at[a, p, pl.ds(b * 64, 64), :], kl_rs.at[a, b])

    spread_keys(0)

    for u in range(6):
        wait(eb.at[p, u], el_rs.at[u])
        wait(vs.at[u], vl_rs.at[u])
        wait(px.at[p, u], pl_rs.at[u])
    row16 = lax.broadcasted_iota(jnp.int32, (16, 1024), 0)
    extra = jnp.zeros((16, 1024), F32)
    for u in range(6):
        extra = jnp.where(row16 == u, vs[u], extra)
    eb[p, 6] = extra.astype(BF)
    spread_embed(0)

    @pl.when(source)
    def _():
        wait(wpart, part_rs.at[0])
        wait(vpart, part_rs.at[1])
        wait(ppart, part_rs.at[2])
        own = pixp[...]
        other = ppart[...]
        for k in range(4):
            for n in range(2):
                lo = k * 1024 + n * 512
                w_own = jnp.where(c == 0, ew[:, lo : lo + 512], ew[:, 4096 + lo : 4096 + lo + 512])
                b_own = jnp.where(c == 0, vf[k, :, n * 512 : (n + 1) * 512], vf[4 + k, :, n * 512 : (n + 1) * 512])
                emb[0, :, lo : lo + 512] = (dot(own, w_own, ((1,), (0,))) + b_own).astype(BF)
                emb[1, :, lo : lo + 512] = (
                    dot(other, wpart[:, lo : lo + 512], ((1,), (0,))) + vpart[k, :, n * 512 : (n + 1) * 512]
                ).astype(BF)

    spread_keys(1)
    spread_keys(2)
    spread_embed(1)
    spread_keys(3)
    spread_keys(4)

    tail_sends = []

    @pl.when(source)
    def _():
        keys = kq[...].reshape(4096, 128)
        lps[...] = dot(emb[1], keys, ((1,), (0,)))
        tail_sends.append(send(lps, lpr, lp_rs.at[0], partner, lambda: lps))
        mine = dot(emb[0], keys, ((1,), (0,)))
        wait(lpr, lp_rs.at[0])
        turned = (mine + lpr[...]).T
        scaled = (turned[:64] + turned[64:]) / jnp.sqrt(jnp.float32(HD))
        for k in range(16):
            for n in range(2):
                ls[k, n * 4 : (n + 1) * 4, :] = scaled[4 * k : 4 * k + 4, n * 128 : (n + 1) * 128]
        pltpu.make_async_copy(ls.at[p], lq.at[p], lq_rs.at[0]).start()
        for k in range(1, 16):
            pd = wrap16(p + k)
            tail_sends.append(send(ls.at[pd], lq.at[p], lq_rs.at[0], dev(s, pd), lambda: ls.at[0]))

    spread_embed(2)

    @pl.when(source)
    def _():
        wait(lq, lq_rs.at[0])
        pltpu.make_async_copy(lq, lr.at[s], lr_rs.at[s]).start()
        for sd in line_ids:
            tail_sends.append(send(lq, lr.at[s], lr_rs.at[s], dev(sd, p), lambda: lq))

    pltpu.make_async_copy(ow_ref.at[:, own_col], ow.at[s], ow_rs.at[s]).start()
    for sd in line_ids:
        col = pl.ds(pl.multiple_of(sd * 1024, 1024), 1024)
        send(ow_ref.at[:, col], ow.at[s], ow_rs.at[s], dev(sd, p))

    for u in range(6):
        wait(lr.at[u], lr_rs.at[u])
    live = [(u, k) for u in range(6) for k in range(16) if (u // 2) * 32 + 2 * k + u % 2 < V]
    top = lr[0, 0]
    for u, k in live[1:]:
        top = jnp.maximum(top, lr[u, k])
    norm = jnp.zeros((8, 128), F32)
    for u, k in live:
        e = jnp.exp(lr[u, k] - top)
        aw[u, k] = e
        norm = norm + e
    for u in range(6):
        for k in range(16):
            if (u, k) in live:
                aw[u, k] = (aw[u, k] / norm).astype(BF).astype(F32)
            else:
                aw[u, k] = jnp.zeros((8, 128), F32)

    for k in range(8):
        wait(vt.at[k], vt_rs.at[k])
    row_n = lax.broadcasted_iota(jnp.int32, (16, 128), 0)

    def work(item):
        values = dot(vt[...].reshape(512, 1024), eb[item].reshape(128, 1024), ((1,), (1,)))
        evt[:, :, pl.ds(pl.multiple_of(item * 128, 128), 128)] = values.astype(BF).reshape(4, 128, 128)
        for n in range(2):
            lanes = slice(n * 128, (n + 1) * 128)
            tails = [jnp.zeros((16, 128), F32) for _ in range(4)]
            for u in range(6):
                pixel = px[item, u, :, lanes].astype(F32)
                weights = aw[u, item]
                for h in range(4):
                    w = weights[n * 4 + h : n * 4 + h + 1, :]
                    at[h, item, u * 16 : (u + 1) * 16, lanes] = (pixel * w).astype(BF)
                    tails[h] = jnp.where(row_n == u, w, tails[h])
            for h in range(4):
                at[h, item, 96:112, lanes] = tails[h].astype(BF)
                at[h, item, 112:128, lanes] = jnp.zeros((16, 128), BF)

    def work_all(dist):
        found = [(o1, o2) for o1 in OFFSETS for o2 in OFFSETS if abs(o1) + abs(o2) == dist]
        for o1, o2 in found:
            work(place(o1, o2))

    work_all(0)
    work_all(1)
    spread_embed(3)
    work_all(2)
    spread_embed(4)
    work_all(3)
    work_all(4)

    for k in range(1, 5):
        xd = lax.rem(x + k, 4)
        part = dot(evt[xd], at[xd].reshape(2048, 256), ((1,), (0,)))
        hp[2 * xd] = part[:64]
        hp[2 * xd + 1] = part[64:]
        if k < 4:
            for cd in range(2):
                send(hp.at[2 * xd + cd], hr.at[s], hr_rs.at[s], dev(2 * xd + cd, p))
        else:
            send(hp.at[2 * x + 1 - c], hr.at[s], hr_rs.at[s], partner)
    heads = hp[s]
    for sd in line_ids:
        wait(hr.at[sd], hr_rs.at[sd])
        heads = heads + hr[sd]
    hg[s] = heads.astype(BF)
    for sd in line_ids:
        send(hg.at[s], hg.at[s], hg_rs.at[s], dev(sd, p))
    for sd in line_ids:
        wait(hg.at[sd], hg_rs.at[sd])
    for k in range(8):
        wait(ow.at[k], ow_rs.at[k])

    mixed = dot(hg[...].reshape(512, 256), ow[...].reshape(512, 1024), ((0,), (0,)))
    ms[...] = mixed.astype(BF).reshape(16, 16, 1024)
    pltpu.make_async_copy(ms.at[p], mr.at[p], mr_rs.at[0]).start()
    for k in range(1, 16):
        pd = wrap16(p + k)
        send(ms.at[pd], mr.at[p], mr_rs.at[0], dev(s, pd))
    wait(mr, mr_rs.at[0])
    final = mr[0].astype(F32)
    for k in range(1, 16):
        final = final + mr[k].astype(F32)
    for k in range(8):
        ob[k] = final[2 * k : 2 * k + 2, :]
    pltpu.make_async_copy(ob.at[s], obr.at[s], ob_rs.at[s]).start()
    for sd in line_ids:
        send(ob.at[sd], obr.at[s], ob_rs.at[s], dev(sd, p))
    for k in range(8):
        wait(obr.at[k], ob_rs.at[k])
        out_ref[:, k * 1024 : (k + 1) * 1024] = obr[k].astype(BF)

    for ref, sem in pending:
        wait(ref, sem)
    for cond, pair in key_sends:

        @pl.when(cond)
        def _():
            drain([pair])

    @pl.when(source)
    def _():
        drain(first_sends)
        drain(k_sends)
        drain(tail_sends)


def body(pixels, embed_w, var_embed, key_w, query, value_t, out_w):
    vmem = pl.BlockSpec(memory_space=pltpu.VMEM)
    hbm = pl.BlockSpec(memory_space=pl.ANY)
    dma = pltpu.SemaphoreType.DMA
    return pl.pallas_call(
        kernel,
        out_shape=jax.ShapeDtypeStruct((2, D), BF),
        in_specs=[vmem, hbm, vmem, hbm, vmem, hbm, hbm],
        out_specs=vmem,
        scratch_shapes=[
            pltpu.VMEM((64, D), BF),
            pltpu.VMEM((16, D), BF),
            pltpu.VMEM((8, 1, 1024), F32),
            pltpu.VMEM((256, 16), BF),
            pltpu.VMEM((16, 256), BF),
            pltpu.VMEM((16, 4096), BF),
            pltpu.VMEM((4, 1, 1024), F32),
            pltpu.VMEM((256, 16), BF),
            pltpu.VMEM((2, 256, 4096), BF),
            pltpu.VMEM((64, 128), BF),
            pltpu.VMEM((2, 16, 128, 128), BF),
            pltpu.VMEM((16, 8, 16, 1024), BF),
            pltpu.VMEM((6, 1, 1024), F32),
            pltpu.VMEM((16, 6, 16, 256), BF),
            pltpu.VMEM((8, 64, 1024), BF),
            pltpu.VMEM((8, 64, 1024), BF),
            pltpu.VMEM((256, 128), F32),
            pltpu.VMEM((256, 128), F32),
            pltpu.VMEM((16, 8, 128), F32),
            pltpu.VMEM((16, 8, 128), F32),
            pltpu.VMEM((6, 16, 8, 128), F32),
            pltpu.VMEM((6, 16, 8, 128), F32),
            pltpu.VMEM((4, 128, 2048), BF),
            pltpu.VMEM((4, 16, 128, 256), BF),
            pltpu.VMEM((8, 64, 256), F32),
            pltpu.VMEM((8, 64, 256), F32),
            pltpu.VMEM((8, 64, 256), BF),
            pltpu.VMEM((16, 16, 1024), BF),
            pltpu.VMEM((16, 16, 1024), BF),
            pltpu.VMEM((8, 2, 1024), F32),
            pltpu.VMEM((8, 2, 1024), F32),
            dma((2,)),
            dma((220,)),
            dma((6,)),
            dma((6,)),
            dma((6,)),
            dma((3,)),
            dma((2, 2)),
            dma((8,)),
            dma((8,)),
            dma((2, 16)),
            dma((2, 16)),
            dma((2, 16)),
            dma((1,)),
            dma((1,)),
            dma((6,)),
            dma((8,)),
            dma((8,)),
            dma((1,)),
            dma((8,)),
        ],
        compiler_params=pltpu.CompilerParams(collective_id=0, has_side_effects=True, vmem_limit_bytes=56 * 1024 * 1024),
    )(pixels, embed_w, var_embed, key_w, query.reshape(1, D), value_t, out_w)


def solution(mesh):
    placed = (
        P("dev", None, None),
        P("dev", None, None),
        P("dev", None),
        P("dev", None),
        P(),
        P("dev", None),
        P("dev", None),
    )
    return jax.shard_map(body, mesh=mesh, in_specs=placed, out_specs=P("dev", None), check_vma=False)
```

time: 382 us -> 110 us (0.29)
  local copies, waits for them, and re-layouts: 115 us -> 2.82 us
  Pallas kernels: 0 us -> 106 us
  blocking collectives: 98.3 us -> 0 us
  waiting for transfers between devices: 83.2 us -> 0 us
  matrix products: 31.1 us -> 0 us
  other arithmetic: 27.9 us -> 0 us
  between operations: 13.5 us -> 0.01 us
  starting transfers between devices: 12 us -> 0 us
    pallas_call x0 -> x1, Pallas kernels: none -> 106 us  [body(): pl.pallas_call(kernel, out_shape=jax.ShapeDtypeStruct((2, D), BF), in_spe...]
    all_to_all x3 -> x0, blocking collectives: 98.3 us -> none  [the longest x1 58.7 us: body(): lax.all_to_all(spread, 'dev', split_axis=1, concat_axis=0, tiled=True)]
    all_to_all x1 -> x0, waiting for transfers between devices: 50.3 us -> none  [body(): lax.all_to_all(own_embed, 'dev', split_axis=1, concat_axis=0, tiled=True)]
    all_to_all x6 -> x0, local copies, waits for them, and re-layouts: 42.3 us -> none  [the longest x2 35.3 us: body(): lax.all_to_all(own_embed, 'dev', split_axis=1, concat_axis=0, tiled=True)]
    all_gather x2 -> x0, waiting for transfers between devices: 32.9 us -> none  [the longest x1 32.9 us: body(): lax.all_gather(value_heads, 'dev', axis=1, tiled=True)]
    unnamed x13 -> x2, local copies, waits for them, and re-layouts: 34 us -> 2.82 us
    dot_general x6 -> x0, matrix products: 31.1 us -> none  [the longest x1 11 us: body(): jnp.einsum('vtd,dh->vth', grouped.astype(jnp.float32), keyq, precision=la...]
    unnamed x1 -> x0, other arithmetic: 26.9 us -> none
  transfers between devices with their start and end apart: 3 -> 0, of which waited for: 2 -> 0; matrix products, arithmetic and copies ran while one was open for 15% -> 0% of each run, Pallas kernels for 0% -> 0%
where the time goes in v1:
time: 110 us; the launch traced here: 109 us
  Pallas kernels  106 us (96%)
  local copies, waits for them, and re-layouts  2.82 us (3%)
    pallas_call x1, Pallas kernels, body(): pl.pallas_call(kernel, out_shape=jax.ShapeDtypeStruct((2, D), BF), in_spe...  106 us
    unnamed x2, local copies, waits for them, and re-layouts  2.82 us

profile of v1, /device:TPU:1, one launch (start us, length us, event | category | flops | bytes accessed | tf_op | source)
XLA Modules:
  0.0 109.3 jit_solution(4922162942602994722)
XLA Ops:
  0.0 1.4 %copy.8.pix_ref = bf16[1,256,16]{2,1,0:T(8,128)(2,1)} copy(bf16[1,256,16]{1,2,0:T(8,128)(2,1)} %param.7) | data formatting | bytes 16384 | tf_op args[0]
  1.4 106.4 %shard_map.73 = bf16[2,8192]{1,0:T(2,128)(2,1)} custom-call(bf16[1,256,16]{2,1,0:T(8,128)(2,1)} %copy.8.pix_ref, bf16[1,16,8192]{2,1,0:T(8,128)(2,1)} %ew_ref.1, bf16[1,8192]{1,0:T(2,128)(2,1)} %var_ref.1, bf16[64,8192]{1,0:T(8,128)(2,1)} %kw_ref.1, f32[1,8192]{1,0:T(1,128)} %bitcast.1, bf16[64,8192]{1,0:T(8,128)(2,1)} %vt_ref.1, bf16[64,8192]{1,0:T(8,128)(2,1)} %ow_ref.1), custom_call_target="tpu_custom_call" | custom-call | tf_op jit(solution)/shard_map/pallas_call | solution.py:446
  107.9 1.4 %copy.10 = bf16[2,8192]{1,0:T(2,128)(2,1)} copy(bf16[2,8192]{1,0:T(2,128)(2,1)} %shard_map.73) | data formatting | bytes 65536

commit v2 on v1

--- a/solution.py
+++ b/solution.py
@@ -28,6 +28,9 @@
     vt_ref,
     ow_ref,
     out_ref,
+    q,
+    pix,
+    var,
     kw,
     ew,
     vf,
@@ -58,7 +61,6 @@
     ms,
     mr,
     ob,
-    obr,
     loc_sem,
     ssem,
     el_rs,
@@ -71,6 +73,7 @@
     kag_rs,
     eag_rs,
     pag_rs,
+    pair_rs,
     lp_rs,
     lq_rs,
     lr_rs,
@@ -104,7 +107,7 @@
     def send(src, dst, rs, d, like=None):
         number = counter[0]
         counter[0] += 1
-        sem = ssem.at[number]
+        sem = ssem.at[0]
         pltpu.make_async_remote_copy(
             src_ref=src, dst_ref=dst, send_sem=sem, recv_sem=rs, device_id=(d,), device_id_type=MESH
         ).start()
@@ -117,68 +120,49 @@
 
     def drain(pairs):
         for like, number in pairs:
-            wait(like(), ssem.at[number])
+            wait(like(), ssem.at[0])
 
     barrier = pltpu.get_barrier_semaphore()
     for k in range(1, 8):
         pl.semaphore_signal(barrier, inc=1, device_id=(dev(wrap8(s + k), p),), device_id_type=MESH)
     for k in range(1, 16):
         pl.semaphore_signal(barrier, inc=1, device_id=(dev(s, wrap16(p + k)),), device_id_type=MESH)
-    kw_in = pltpu.make_async_copy(kw_ref, kw, loc_sem.at[0])
-    kw_in.start()
-    ew_in = pltpu.make_async_copy(ew_ref.at[0], ew, loc_sem.at[1])
-    ew_in.start()
+    loads = [
+        pltpu.make_async_copy(src, dst, loc_sem.at[i])
+        for i, (src, dst) in enumerate(
+            ((q_ref, q), (kw_ref, kw), (pix_ref.at[0], pix), (var_ref, var), (ew_ref.at[0], ew))
+        )
+    ]
+    for load in loads:
+        load.start()
 
     pos = lax.broadcasted_iota(jnp.int32, (256, 256), 0)
     tok = lax.broadcasted_iota(jnp.int32, (256, 256), 1)
     want = lax.div(lax.rem(pos, 16), 4) * 64 + lax.div(pos, 16) * 4 + lax.rem(pos, 4)
     perm = jnp.where(tok == want, 1.0, 0.0).astype(BF)
-    ordered = dot(perm, pix_ref[0], ((1,), (0,))).astype(BF)
-    pixp[...] = ordered
-    eye = jnp.where(
-        lax.broadcasted_iota(jnp.int32, (16, 16), 0) == lax.broadcasted_iota(jnp.int32, (16, 16), 1), 1.0, 0.0
-    ).astype(BF)
-    pixt[...] = dot(eye, ordered, ((1,), (1,))).astype(BF)
-    for k in range(8):
-        vf[k] = var_ref[:, k * 1024 : (k + 1) * 1024].astype(F32)
-    eb[:, 7] = jnp.zeros((16, 16, 1024), BF)
-    ew_in.wait()
-    pl.semaphore_wait(barrier, 22)
-
-    half = pl.multiple_of((1 - c) * 4096, 4096)
-    first_sends = []
-    line_ids = [wrap8(s + k) for k in range(1, 8)]
-
-    @pl.when(source)
-    def _():
-        first_sends.append(send(ew.at[:, pl.ds(half, 4096)], wpart, part_rs.at[0], partner, lambda: ew.at[:, 0:4096]))
-        first_sends.append(send(vf.at[pl.ds(4 * (1 - c), 4)], vpart, part_rs.at[1], partner, lambda: vf.at[0:4]))
-        first_sends.append(send(pixp, ppart, part_rs.at[2], partner, lambda: pixp))
-        pltpu.make_async_copy(ew.at[:, pl.ds(pl.multiple_of(s * 1024, 1024), 1024)], eb.at[p, s], el_rs.at[s]).start()
-        pltpu.make_async_copy(vf.at[s], vs.at[s], vl_rs.at[s]).start()
-        pltpu.make_async_copy(pixt, px.at[p, s], pl_rs.at[s]).start()
-        for sd in line_ids:
-            col = pl.ds(pl.multiple_of(sd * 1024, 1024), 1024)
-            first_sends.append(send(ew.at[:, col], eb.at[p, s], el_rs.at[s], dev(sd, p), lambda: ew.at[:, 0:1024]))
-            first_sends.append(send(vf.at[sd], vs.at[s], vl_rs.at[s], dev(sd, p), lambda: vf.at[0]))
-            first_sends.append(send(pixt, px.at[p, s], pl_rs.at[s], dev(sd, p), lambda: pixt))
-
-    own_col = pl.ds(pl.multiple_of(s * 1024, 1024), 1024)
-    pltpu.make_async_copy(vt_ref.at[:, own_col], vt.at[s], vt_rs.at[s]).start()
-    for sd in line_ids:
-        col = pl.ds(pl.multiple_of(sd * 1024, 1024), 1024)
-        send(vt_ref.at[:, col], vt.at[s], vt_rs.at[s], dev(sd, p))
-
-    kw_in.wait()
+    eb[:, 104:128, :] = jnp.zeros((16, 24, 1024), BF)
+
+    loads[0].wait()
+    loads[1].wait()
     lane = lax.broadcasted_iota(jnp.int32, (64, 128), 1)
     folded = jnp.where(lane < 64, lane, lane - 64)
     acc = jnp.zeros((64, 128), F32)
     for h in range(HEADS):
         cut = slice(h * HD, (h + 1) * HD)
-        total = jnp.sum(kw[:, cut].astype(F32) * q_ref[:, cut], axis=1, keepdims=True)
+        total = jnp.sum(kw[:, cut].astype(F32) * q[:, cut], axis=1, keepdims=True)
         acc = jnp.where(folded == (h % 16) * 4 + h // 16, total, acc)
     high = acc.astype(BF).astype(F32)
     kqs[...] = jnp.where(lane < 64, high, acc - high).astype(BF)
+
+    loads[2].wait()
+    pixt[...] = dot(pix[...], perm, ((1,), (1,))).astype(BF)
+    pixp[...] = dot(perm, pix[...], ((1,), (1,))).astype(BF)
+    loads[3].wait()
+    for k in range(8):
+        vf[k] = var[:, k * 1024 : (k + 1) * 1024].astype(F32)
+    loads[4].wait()
+
+    pl.semaphore_wait(barrier, 22)
 
     key_half = lax.rem(x, 2)
     key_core = lax.div(x, 2)
@@ -187,7 +171,6 @@
         target = dev(2 * xd + key_core, p)
         dst = kq.at[key_half, p, pl.ds(pl.multiple_of(c * 64, 64), 64), :]
         sem = kl_rs.at[key_half, c]
-
         away = target != me
 
         @pl.when(away)
@@ -198,8 +181,45 @@
         def _():
             pltpu.make_async_copy(kqs, dst, sem).start()
 
+    half = pl.multiple_of((1 - c) * 4096, 4096)
+    first_sends = []
+    line_ids = [wrap8(s + k) for k in range(1, 8)]
+
+    @pl.when(source)
+    def _():
+        first_sends.append(send(ew.at[:, pl.ds(half, 4096)], wpart, part_rs.at[0], partner, lambda: ew.at[:, 0:4096]))
+        first_sends.append(send(vf.at[pl.ds(4 * (1 - c), 4)], vpart, part_rs.at[1], partner, lambda: vf.at[0:4]))
+        first_sends.append(send(pixp, ppart, part_rs.at[2], partner, lambda: pixp))
+        row = pl.ds(pl.multiple_of(s * 16, 16), 16)
+        pltpu.make_async_copy(
+            ew.at[:, pl.ds(pl.multiple_of(s * 1024, 1024), 1024)], eb.at[p, row, :], el_rs.at[s]
+        ).start()
+        pltpu.make_async_copy(vf.at[s], vs.at[s], vl_rs.at[s]).start()
+        own_lanes = pl.ds(pl.multiple_of(c * 128, 128), 128)
+        pltpu.make_async_copy(pixt.at[:, own_lanes], px.at[p, s, :, own_lanes], pl_rs.at[s]).start()
+        for sd in line_ids:
+            col = pl.ds(pl.multiple_of(sd * 1024, 1024), 1024)
+            lanes = pl.ds(pl.multiple_of(lax.rem(sd, 2) * 128, 128), 128)
+            first_sends.append(
+                send(ew.at[:, col], eb.at[p, row, :], el_rs.at[s], dev(sd, p), lambda: ew.at[:, 0:1024])
+            )
+            first_sends.append(send(vf.at[sd], vs.at[s], vl_rs.at[s], dev(sd, p), lambda: vf.at[0]))
+            first_sends.append(
+                send(pixt.at[:, lanes], px.at[p, s, :, lanes], pl_rs.at[s], dev(sd, p), lambda: pixt.at[:, 0:128])
+            )
+
+    own_col = pl.ds(pl.multiple_of(s * 1024, 1024), 1024)
+    pltpu.make_async_copy(vt_ref.at[:, own_col], vt.at[s], vt_rs.at[s]).start()
+    for sd in line_ids:
+        col = pl.ds(pl.multiple_of(sd * 1024, 1024), 1024)
+        send(vt_ref.at[:, col], vt.at[s], vt_rs.at[s], dev(sd, p))
+
     def place(oz, oy):
         return lax.rem(z + oz + 4, 4) * 4 + lax.rem(y + oy + 4, 4)
+
+    def hand_over(half_id, item):
+        ref = pixel_block(half_id, item)
+        send(ref, ref, pair_rs.at[half_id, item], partner)
 
     def spread(dist, half_id, payloads, conditional=None):
         for o1 in OFFSETS:
@@ -211,6 +231,8 @@
                 if dist > 0:
                     for ref_of, sems in payloads:
                         wait(ref_of(half_id, item), sems.at[half_id, item])
+                if conditional is None:
+                    hand_over(half_id, item)
                 sign = 1 if half_id == 0 else -1
                 moves = []
                 if o2 == 0:
@@ -237,10 +259,10 @@
         return kq.at[half_id, item]
 
     def embed_block(half_id, item):
-        return eb.at[item, pl.ds(0, 7), :, pl.ds(half_id * 512, 512)]
+        return eb.at[item, pl.ds(0, 104), pl.ds(half_id * 512, 512)]
 
     def pixel_block(half_id, item):
-        return px.at[item, :, :, pl.ds(half_id * 128, 128)]
+        return px.at[item, pl.ds(3 * half_id, 3), :, pl.ds(pl.multiple_of(c * 128, 128), 128)]
 
     e_payloads = ((embed_block, eag_rs), (pixel_block, pag_rs))
     k_payloads = ((key_block, kag_rs),)
@@ -252,9 +274,8 @@
             for half_id in (0, 1):
                 spread(dist, half_id, k_payloads, k_sends)
 
-    def spread_embed(dist):
-        for half_id in (0, 1):
-            spread(dist, half_id, e_payloads)
+    def spread_embed(dist, half_id):
+        spread(dist, half_id, e_payloads)
 
     @pl.when(source)
     def _():
@@ -265,15 +286,15 @@
     spread_keys(0)
 
     for u in range(6):
-        wait(eb.at[p, u], el_rs.at[u])
+        wait(eb.at[p, u * 16 : (u + 1) * 16, :], el_rs.at[u])
         wait(vs.at[u], vl_rs.at[u])
-        wait(px.at[p, u], pl_rs.at[u])
-    row16 = lax.broadcasted_iota(jnp.int32, (16, 1024), 0)
-    extra = jnp.zeros((16, 1024), F32)
+        wait(px.at[p, u, :, pl.ds(pl.multiple_of(c * 128, 128), 128)], pl_rs.at[u])
+    row8 = lax.broadcasted_iota(jnp.int32, (8, 1024), 0)
+    extra = jnp.zeros((8, 1024), F32)
     for u in range(6):
-        extra = jnp.where(row16 == u, vs[u], extra)
-    eb[p, 6] = extra.astype(BF)
-    spread_embed(0)
+        extra = jnp.where(row8 == u, vs[u], extra)
+    eb[p, 96:104, :] = extra.astype(BF)
+    spread_embed(0, 0)
 
     @pl.when(source)
     def _():
@@ -293,9 +314,11 @@
                 ).astype(BF)
 
     spread_keys(1)
+    spread_embed(0, 1)
     spread_keys(2)
-    spread_embed(1)
+    spread_embed(1, 0)
     spread_keys(3)
+    spread_embed(1, 1)
     spread_keys(4)
 
     tail_sends = []
@@ -317,7 +340,8 @@
             pd = wrap16(p + k)
             tail_sends.append(send(ls.at[pd], lq.at[p], lq_rs.at[0], dev(s, pd), lambda: ls.at[0]))
 
-    spread_embed(2)
+    spread_embed(2, 0)
+    spread_embed(2, 1)
 
     @pl.when(source)
     def _():
@@ -330,6 +354,23 @@
     for sd in line_ids:
         col = pl.ds(pl.multiple_of(sd * 1024, 1024), 1024)
         send(ow_ref.at[:, col], ow.at[s], ow_rs.at[s], dev(sd, p))
+
+    spread_embed(3, 0)
+    spread_embed(3, 1)
+
+    for k in range(8):
+        wait(vt.at[k], vt_rs.at[k])
+
+    def places(dist):
+        return [place(o1, o2) for o1 in OFFSETS for o2 in OFFSETS if abs(o1) + abs(o2) == dist]
+
+    def value_columns(dist):
+        for item in places(dist):
+            values = dot(vt[...].reshape(512, 1024), eb[item], ((1,), (1,)))
+            evt[:, :, pl.ds(pl.multiple_of(item * 128, 128), 128)] = values.astype(BF).reshape(4, 128, 128)
+
+    for dist in range(4):
+        value_columns(dist)
 
     for u in range(6):
         wait(lr.at[u], lr_rs.at[u])
@@ -349,43 +390,40 @@
             else:
                 aw[u, k] = jnp.zeros((8, 128), F32)
 
-    for k in range(8):
-        wait(vt.at[k], vt_rs.at[k])
     row_n = lax.broadcasted_iota(jnp.int32, (16, 128), 0)
 
-    def work(item):
-        values = dot(vt[...].reshape(512, 1024), eb[item].reshape(128, 1024), ((1,), (1,)))
-        evt[:, :, pl.ds(pl.multiple_of(item * 128, 128), 128)] = values.astype(BF).reshape(4, 128, 128)
-        for n in range(2):
-            lanes = slice(n * 128, (n + 1) * 128)
-            tails = [jnp.zeros((16, 128), F32) for _ in range(4)]
-            for u in range(6):
-                pixel = px[item, u, :, lanes].astype(F32)
-                weights = aw[u, item]
+    def weigh(dist):
+        for item in places(dist):
+            other = pl.ds(pl.multiple_of((1 - c) * 128, 128), 128)
+            for half_id in (0, 1):
+                wait(px.at[item, pl.ds(3 * half_id, 3), :, other], pair_rs.at[half_id, item])
+            for n in range(2):
+                lanes = slice(n * 128, (n + 1) * 128)
+                tails = [jnp.zeros((16, 128), F32) for _ in range(4)]
+                for u in range(6):
+                    pixel = px[item, u, :, lanes].astype(F32)
+                    weights = aw[u, item]
+                    for h in range(4):
+                        w = weights[n * 4 + h : n * 4 + h + 1, :]
+                        at[h, item, u * 16 : (u + 1) * 16, lanes] = (pixel * w).astype(BF)
+                        tails[h] = jnp.where(row_n == u, w, tails[h])
                 for h in range(4):
-                    w = weights[n * 4 + h : n * 4 + h + 1, :]
-                    at[h, item, u * 16 : (u + 1) * 16, lanes] = (pixel * w).astype(BF)
-                    tails[h] = jnp.where(row_n == u, w, tails[h])
-            for h in range(4):
-                at[h, item, 96:112, lanes] = tails[h].astype(BF)
-                at[h, item, 112:128, lanes] = jnp.zeros((16, 128), BF)
-
-    def work_all(dist):
-        found = [(o1, o2) for o1 in OFFSETS for o2 in OFFSETS if abs(o1) + abs(o2) == dist]
-        for o1, o2 in found:
-            work(place(o1, o2))
-
-    work_all(0)
-    work_all(1)
-    spread_embed(3)
-    work_all(2)
-    spread_embed(4)
-    work_all(3)
-    work_all(4)
+                    at[h, item, 96:112, lanes] = tails[h].astype(BF)
+                    at[h, item, 112:128, lanes] = jnp.zeros((16, 128), BF)
+
+    for dist in range(4):
+        weigh(dist)
+    spread_embed(4, 0)
+    spread_embed(4, 1)
+    value_columns(4)
+    weigh(4)
 
     for k in range(1, 5):
         xd = lax.rem(x + k, 4)
         part = dot(evt[xd], at[xd].reshape(2048, 256), ((1,), (0,)))
+        if k == 4:
+            heads = jnp.where(c == 0, part[:64], part[64:])
+        part = part.astype(BF)
         hp[2 * xd] = part[:64]
         hp[2 * xd + 1] = part[64:]
         if k < 4:
@@ -393,10 +431,9 @@
                 send(hp.at[2 * xd + cd], hr.at[s], hr_rs.at[s], dev(2 * xd + cd, p))
         else:
             send(hp.at[2 * x + 1 - c], hr.at[s], hr_rs.at[s], partner)
-    heads = hp[s]
     for sd in line_ids:
         wait(hr.at[sd], hr_rs.at[sd])
-        heads = heads + hr[sd]
+        heads = heads + hr[sd].astype(F32)
     hg[s] = heads.astype(BF)
     for sd in line_ids:
         send(hg.at[s], hg.at[s], hg_rs.at[s], dev(sd, p))
@@ -417,12 +454,11 @@
         final = final + mr[k].astype(F32)
     for k in range(8):
         ob[k] = final[2 * k : 2 * k + 2, :]
-    pltpu.make_async_copy(ob.at[s], obr.at[s], ob_rs.at[s]).start()
+    pltpu.make_async_copy(ob.at[s], out_ref.at[s], ob_rs.at[s]).start()
     for sd in line_ids:
-        send(ob.at[sd], obr.at[s], ob_rs.at[s], dev(sd, p))
+        send(ob.at[sd], out_ref.at[s], ob_rs.at[s], dev(sd, p))
     for k in range(8):
-        wait(obr.at[k], ob_rs.at[k])
-        out_ref[:, k * 1024 : (k + 1) * 1024] = obr[k].astype(BF)
+        wait(out_ref.at[k], ob_rs.at[k])
 
     for ref, sem in pending:
         wait(ref, sem)
@@ -440,15 +476,17 @@
 
 
 def body(pixels, embed_w, var_embed, key_w, query, value_t, out_w):
-    vmem = pl.BlockSpec(memory_space=pltpu.VMEM)
     hbm = pl.BlockSpec(memory_space=pl.ANY)
     dma = pltpu.SemaphoreType.DMA
-    return pl.pallas_call(
+    slices = pl.pallas_call(
         kernel,
-        out_shape=jax.ShapeDtypeStruct((2, D), BF),
-        in_specs=[vmem, hbm, vmem, hbm, vmem, hbm, hbm],
-        out_specs=vmem,
+        out_shape=jax.ShapeDtypeStruct((8, 2, 1024), F32),
+        in_specs=[hbm] * 7,
+        out_specs=hbm,
         scratch_shapes=[
+            pltpu.VMEM((1, D), F32),
+            pltpu.VMEM((16, 256), BF),
+            pltpu.VMEM((1, D), BF),
             pltpu.VMEM((64, D), BF),
             pltpu.VMEM((16, D), BF),
             pltpu.VMEM((8, 1, 1024), F32),
@@ -460,7 +498,7 @@
             pltpu.VMEM((2, 256, 4096), BF),
             pltpu.VMEM((64, 128), BF),
             pltpu.VMEM((2, 16, 128, 128), BF),
-            pltpu.VMEM((16, 8, 16, 1024), BF),
+            pltpu.VMEM((16, 128, 1024), BF),
             pltpu.VMEM((6, 1, 1024), F32),
             pltpu.VMEM((16, 6, 16, 256), BF),
             pltpu.VMEM((8, 64, 1024), BF),
@@ -473,15 +511,14 @@
             pltpu.VMEM((6, 16, 8, 128), F32),
             pltpu.VMEM((4, 128, 2048), BF),
             pltpu.VMEM((4, 16, 128, 256), BF),
-            pltpu.VMEM((8, 64, 256), F32),
-            pltpu.VMEM((8, 64, 256), F32),
+            pltpu.VMEM((8, 64, 256), BF),
+            pltpu.VMEM((8, 64, 256), BF),
             pltpu.VMEM((8, 64, 256), BF),
             pltpu.VMEM((16, 16, 1024), BF),
             pltpu.VMEM((16, 16, 1024), BF),
             pltpu.VMEM((8, 2, 1024), F32),
-            pltpu.VMEM((8, 2, 1024), F32),
-            dma((2,)),
-            dma((220,)),
+            dma((5,)),
+            dma((1,)),
             dma((6,)),
             dma((6,)),
             dma((6,)),
@@ -489,6 +526,7 @@
             dma((2, 2)),
             dma((8,)),
             dma((8,)),
+            dma((2, 16)),
             dma((2, 16)),
             dma((2, 16)),
             dma((2, 16)),
@@ -501,7 +539,8 @@
             dma((8,)),
         ],
         compiler_params=pltpu.CompilerParams(collective_id=0, has_side_effects=True, vmem_limit_bytes=56 * 1024 * 1024),
-    )(pixels, embed_w, var_embed, key_w, query.reshape(1, D), value_t, out_w)
+    )(pixels.transpose(0, 2, 1), embed_w, var_embed, key_w, query.reshape(1, D), value_t, out_w)
+    return slices.transpose(1, 0, 2).reshape(2, D).astype(BF)
 
 
 def solution(mesh):

time: 110 us -> 87.8 us (0.80)
  Pallas kernels: 106 us -> 86.1 us
  local copies, waits for them, and re-layouts: 2.82 us -> 0 us
  other arithmetic: 0 us -> 1.48 us
    pallas_call x1, Pallas kernels: 106 us -> 86.1 us  [body(): pl.pallas_call(kernel, out_shape=jax.ShapeDtypeStruct((8, 2, 1024), F32),...]
    unnamed x2 -> x0, local copies, waits for them, and re-layouts: 2.82 us -> none
    convert_element_type x0 -> x1, other arithmetic: none -> 1.48 us  [body(): return slices.transpose(1, 0, 2).reshape(2, D).astype(BF)]
where the time goes in v2:
time: 87.8 us; the launch traced here: 87.6 us
  Pallas kernels  86.1 us (98%)
  other arithmetic  1.48 us (2%)
    pallas_call x1, Pallas kernels, body(): pl.pallas_call(kernel, out_shape=jax.ShapeDtypeStruct((8, 2, 1024), F32),...  86.1 us

profile of v2, /device:TPU:1, one launch (start us, length us, event | category | flops | bytes accessed | tf_op | source)
XLA Modules:
  0.0 87.6 jit_solution(17218564883880680696)
XLA Ops:
  0.0 86.1 %shard_map.73 = f32[8,2,1024]{2,1,0:T(2,128)} custom-call(bf16[1,16,256]{2,1,0:T(8,128)(2,1)} %bitcast.6, bf16[1,16,8192]{2,1,0:T(8,128)(2,1)} %ew_ref.1, bf16[1,8192]{1,0:T(2,128)(2,1)} %var_ref.1, bf16[64,8192]{1,0:T(8,128)(2,1)} %kw_ref.1, f32[1,8192]{1,0:T(1,128)} %bitcast.5, bf16[64,8192]{1,0:T(8,128)(2,1)} %vt_ref.1, bf16[64,8192]{1,0:T(8,128)(2,1)} %ow_ref.1), custom_call_target="tpu_custom_call" | custom-call | tf_op jit(solution)/shard_map/pallas_call | solution.py:481
  86.1 1.5 %convert_element_type.9 = bf16[8,2,1024]{2,1,0:T(2,128)(2,1)} convert(f32[8,2,1024]{2,1,0:T(2,128)} %shard_map.73) | non-fusion elementwise | flops 16384 | bytes 98304 | tf_op jit(solution)/shard_map/convert_element_type | solution.py:543

commit v3 on v2

v3 whole, which is shorter than its diff:
```python
import jax
import jax.numpy as jnp
from jax import lax
from jax.experimental import pallas as pl
from jax.experimental.pallas import tpu as pltpu
from jax.sharding import PartitionSpec as P

D = 8192
HEADS = 64
HD = 128
V = 91
MESH = pl.DeviceIdType.MESH
BF = jnp.bfloat16
F32 = jnp.float32
OFFSETS = (0, -1, 1, 2)


def dot(a, b, dims):
    return lax.dot_general(a, b, (dims, ((), ())), preferred_element_type=F32)


def kernel(
    pix_ref,
    ew_ref,
    var_ref,
    kw_ref,
    q_ref,
    vt_ref,
    ow_ref,
    out_ref,
    q,
    pix,
    var,
    kw,
    ew,
    vf,
    pixt,
    emb,
    kqs,
    kq,
    eb,
    vs,
    px,
    vt,
    ow,
    lp,
    lpr,
    ls,
    lr,
    aw,
    evt,
    at,
    hp,
    hr,
    hg,
    ms,
    mr,
    ob,
    loc_sem,
    ssem,
    el_rs,
    vl_rs,
    pl_rs,
    kq_rs,
    vt_rs,
    ow_rs,
    eag_rs,
    pag_rs,
    pair_rs,
    lp_rs,
    lr_rs,
    aw_rs,
    hr_rs,
    hg_rs,
    mr_rs,
    ob_rs,
):
    me = lax.axis_index("dev")
    x = lax.div(me, 32)
    p = lax.rem(lax.div(me, 2), 16)
    c = lax.rem(me, 2)
    z = lax.div(p, 4)
    y = lax.rem(p, 4)
    s = 2 * x + c
    partner = x * 32 + p * 2 + (1 - c)
    source = x < 3

    def dev(s_, p_):
        return lax.div(s_, 2) * 32 + p_ * 2 + lax.rem(s_, 2)

    def wrap8(v):
        return lax.rem(v + 8, 8)

    def wrap16(v):
        return lax.rem(v + 16, 16)

    pending = []
    counter = [0]

    def send(src, dst, rs, d, like=None):
        number = counter[0]
        counter[0] += 1
        sem = ssem.at[0]
        pltpu.make_async_remote_copy(
            src_ref=src, dst_ref=dst, send_sem=sem, recv_sem=rs, device_id=(d,), device_id_type=MESH
        ).start()
        if like is None:
            pending.append((src, sem))
        return like, number

    def wait(ref, sem):
        pltpu.make_async_copy(ref, ref, sem).wait()

    def drain(pairs):
        for like, number in pairs:
            wait(like(), ssem.at[0])

    barrier = pltpu.get_barrier_semaphore()
    for k in range(1, 8):
        pl.semaphore_signal(barrier, inc=1, device_id=(dev(wrap8(s + k), p),), device_id_type=MESH)
    for k in range(1, 16):
        for core in range(2):
            near = x * 32 + wrap16(p + k) * 2 + core
            pl.semaphore_signal(barrier, inc=1, device_id=(near,), device_id_type=MESH)
    loads = [
        pltpu.make_async_copy(src, dst, loc_sem.at[i])
        for i, (src, dst) in enumerate(
            ((q_ref, q), (kw_ref, kw), (pix_ref.at[0], pix), (var_ref, var), (ew_ref.at[0], ew))
        )
    ]
    for load in loads:
        load.start()

    pos = lax.broadcasted_iota(jnp.int32, (256, 256), 0)
    tok = lax.broadcasted_iota(jnp.int32, (256, 256), 1)
    want = lax.div(lax.rem(pos, 16), 4) * 64 + lax.div(pos, 16) * 4 + lax.rem(pos, 4)
    perm = jnp.where(tok == want, 1.0, 0.0).astype(BF)
    eb[:, 104:128, :] = jnp.zeros((16, 24, 1024), BF)
    ls[...] = jnp.zeros((16, 8, 128), F32)

    loads[0].wait()
    loads[1].wait()
    lane = lax.broadcasted_iota(jnp.int32, (64, 128), 1)
    folded = jnp.where(lane < 64, lane, lane - 64)
    acc = jnp.zeros((64, 128), F32)
    for h in range(HEADS):
        cut = slice(h * HD, (h + 1) * HD)
        total = jnp.sum(kw[:, cut].astype(F32) * q[:, cut], axis=1, keepdims=True)
        acc = jnp.where(folded == h, total, acc)
    high = acc.astype(BF).astype(F32)
    kqs[...] = jnp.where(lane < 64, high, acc - high).astype(BF)

    loads[2].wait()
    pixt[...] = dot(pix[...], perm, ((1,), (1,))).astype(BF)
    loads[3].wait()
    for k in range(8):
        vf[k] = var[:, k * 1024 : (k + 1) * 1024].astype(F32)
    loads[4].wait()

    pl.semaphore_wait(barrier, 37)

    key_core = lax.div(p, 8)
    key_dst = kq.at[lax.rem(p, 8) * 2 + c]
    at_home = key_core == c

    @pl.when(at_home)
    def _():
        pltpu.make_async_copy(kqs, key_dst, kq_rs.at[0]).start()

    across = []

    @pl.when(jnp.logical_not(at_home))
    def _():
        across.append(send(kqs, key_dst, kq_rs.at[0], partner, lambda: kqs))

    for k in range(1, 16):
        send(kqs, key_dst, kq_rs.at[0], x * 32 + wrap16(p + k) * 2 + key_core)

    first_sends = []
    line_ids = [wrap8(s + k) for k in range(1, 8)]

    @pl.when(source)
    def _():
        row = pl.ds(pl.multiple_of(s * 16, 16), 16)
        pltpu.make_async_copy(
            ew.at[:, pl.ds(pl.multiple_of(s * 1024, 1024), 1024)], eb.at[p, row, :], el_rs.at[s]
        ).start()
        pltpu.make_async_copy(vf.at[s], vs.at[s], vl_rs.at[s]).start()
        pltpu.make_async_copy(pixt, px.at[p, s], pl_rs.at[s]).start()
        for sd in line_ids:
            col = pl.ds(pl.multiple_of(sd * 1024, 1024), 1024)
            first_sends.append(
                send(ew.at[:, col], eb.at[p, row, :], el_rs.at[s], dev(sd, p), lambda: ew.at[:, 0:1024])
            )
            first_sends.append(send(vf.at[sd], vs.at[s], vl_rs.at[s], dev(sd, p), lambda: vf.at[0]))
            first_sends.append(send(pixt, px.at[p, s], pl_rs.at[s], dev(sd, p), lambda: pixt))

    own_col = pl.ds(pl.multiple_of(s * 1024, 1024), 1024)
    pltpu.make_async_copy(vt_ref.at[:, own_col], vt.at[s], vt_rs.at[s]).start()

    def hand_values(which):
        for sd in which:
            col = pl.ds(pl.multiple_of(sd * 1024, 1024), 1024)
            send(vt_ref.at[:, col], vt.at[s], vt_rs.at[s], dev(sd, p))

    def place(oz, oy):
        return lax.rem(z + oz + 4, 4) * 4 + lax.rem(y + oy + 4, 4)

    def hand_over(half_id, item):
        ref = pixel_block(half_id, item)
        send(ref, ref, pair_rs.at[half_id, item], partner)

    def spread_embed(dist, half_id):
        for o1 in OFFSETS:
            for o2 in OFFSETS:
                if abs(o1) + abs(o2) != dist:
                    continue
                oy, oz = (o1, o2) if half_id == 0 else (o2, o1)
                item = place(oz, oy)
                if dist > 0:
                    for ref_of, sems in e_payloads:
                        wait(ref_of(half_id, item), sems.at[half_id, item])
                    hand_over(half_id, item)
                sign = 1 if half_id == 0 else -1
                moves = []
                if o2 == 0:
                    if o1 == 0:
                        moves += [(1, 0), (-1, 0)]
                    elif o1 == -sign:
                        moves += [(sign, 0)]
                    moves += [(0, 1), (0, -1)]
                else:
                    f2 = sign if o1 in (0, 2) else -sign
                    if o2 == -f2:
                        moves += [(0, f2)]
                for m1, m2 in moves:
                    my, mz = (m1, m2) if half_id == 0 else (m2, m1)
                    target = dev(s, place(mz, my))
                    for ref_of, sems in e_payloads:
                        ref = ref_of(half_id, item)
                        send(ref, ref, sems.at[half_id, item], target)

    def embed_block(half_id, item):
        return eb.at[item, pl.ds(0, 104), pl.ds(half_id * 512, 512)]

    def pixel_block(half_id, item):
        return px.at[item, pl.ds(3 * half_id, 3), :, pl.ds(pl.multiple_of(c * 128, 128), 128)]

    e_payloads = ((embed_block, eag_rs), (pixel_block, pag_rs))

    for u in range(6):
        wait(eb.at[p, u * 16 : (u + 1) * 16, :], el_rs.at[u])
        wait(vs.at[u], vl_rs.at[u])
        wait(px.at[p, u], pl_rs.at[u])
    row8 = lax.broadcasted_iota(jnp.int32, (8, 1024), 0)
    extra = jnp.zeros((8, 1024), F32)
    for u in range(6):
        extra = jnp.where(row8 == u, vs[u], extra)
    eb[p, 96:104, :] = extra.astype(BF)
    spread_embed(0, 0)
    spread_embed(0, 1)
    hand_values(line_ids[:2])

    one = jnp.where(lax.broadcasted_iota(jnp.int32, (8, 256), 0) == 0, 1.0, 0.0).astype(BF)
    for u in range(6):
        first = jnp.where(row8 == 0, vs[u], 0.0).astype(BF)
        weights = jnp.concatenate([eb[p, u * 16 : (u + 1) * 16, :], first], axis=0)
        pixels = jnp.concatenate([px[p, u], one], axis=0)
        emb[u] = dot(weights, pixels, ((0,), (0,))).astype(BF)
    wait(kq, kq_rs.at[0])
    keys = kq[...].reshape(1024, 128).T
    for u in range(6):
        both = dot(keys, emb[u], ((1,), (0,)))
        both = both[:64] + both[64:]
        for k in range(8):
            h = k % 4
            lp[k, u] = both[h * 16 : (h + 1) * 16, (k // 4) * 128 : (k // 4 + 1) * 128]
    for sd in line_ids:
        send(lp.at[sd], lpr.at[s], lp_rs.at[s], dev(sd, p))

    spread_embed(1, 0)
    spread_embed(1, 1)

    logits = lp[s]
    for sd in line_ids:
        wait(lpr.at[sd], lp_rs.at[sd])
        logits = logits + lpr[sd]
    logits = logits / jnp.sqrt(jnp.float32(HD))
    for u in range(6):
        ls[:, u, :] = logits[u]
    pltpu.make_async_copy(ls.at[p], lr.at[p], lr_rs.at[0]).start()
    for k in range(1, 16):
        pd = wrap16(p + k)
        send(ls.at[pd], lr.at[p], lr_rs.at[0], dev(s, pd))
    hand_values(line_ids[2:])

    spread_embed(2, 0)
    spread_embed(2, 1)

    wait(lr, lr_rs.at[0])
    place_id = lax.broadcasted_iota(jnp.int32, (16, 8, 128), 0)
    slot_id = lax.broadcasted_iota(jnp.int32, (16, 8, 128), 1)
    variable = lax.div(slot_id, 2) * 32 + place_id * 2 + lax.rem(slot_id, 2)
    live = jnp.logical_and(slot_id < 6, variable < V)
    logits = jnp.where(live, lr[...], -1e30)
    top = jnp.max(jnp.max(logits, axis=0), axis=0, keepdims=True)
    weights = jnp.where(live, jnp.exp(logits - top), 0.0)
    norm = jnp.sum(jnp.sum(weights, axis=0), axis=0, keepdims=True)
    aw[s] = (weights / norm).astype(BF)
    for sd in line_ids:
        send(aw.at[s], aw.at[s], aw_rs.at[s], dev(sd, p))

    pltpu.make_async_copy(ow_ref.at[:, own_col], ow.at[s], ow_rs.at[s]).start()
    for sd in line_ids:
        col = pl.ds(pl.multiple_of(sd * 1024, 1024), 1024)
        send(ow_ref.at[:, col], ow.at[s], ow_rs.at[s], dev(sd, p))

    for k in range(8):
        wait(vt.at[k], vt_rs.at[k])

    def places(dist):
        return [place(o1, o2) for o1 in OFFSETS for o2 in OFFSETS if abs(o1) + abs(o2) == dist]

    def value_columns(dist):
        for item in places(dist):
            values = dot(vt[...].reshape(512, 1024), eb[item], ((1,), (1,)))
            evt[:, :, pl.ds(pl.multiple_of(item * 128, 128), 128)] = values.astype(BF).reshape(4, 128, 128)

    value_columns(0)
    value_columns(1)
    spread_embed(3, 0)
    spread_embed(3, 1)
    value_columns(2)
    value_columns(3)

    for sd in line_ids:
        wait(aw.at[sd], aw_rs.at[sd])

    row_n = lax.broadcasted_iota(jnp.int32, (16, 128), 0)

    def weigh(dist):
        for item in places(dist):
            other = pl.ds(pl.multiple_of((1 - c) * 128, 128), 128)
            for half_id in (0, 1):
                if dist > 0:
                    wait(px.at[item, pl.ds(3 * half_id, 3), :, other], pair_rs.at[half_id, item])
            for n in range(2):
                lanes = slice(n * 128, (n + 1) * 128)
                tails = [jnp.zeros((16, 128), F32) for _ in range(4)]
                tiles = [aw[n * 4 + h, item].astype(F32) for h in range(4)]
                for u in range(6):
                    pixel = px[item, u, :, lanes].astype(F32)
                    for h in range(4):
                        w = tiles[h][u : u + 1, :]
                        at[h, item, u * 16 : (u + 1) * 16, lanes] = (pixel * w).astype(BF)
                        tails[h] = jnp.where(row_n == u, w, tails[h])
                for h in range(4):
                    at[h, item, 96:112, lanes] = tails[h].astype(BF)
                    at[h, item, 112:128, lanes] = jnp.zeros((16, 128), BF)

    for dist in range(4):
        weigh(dist)
    spread_embed(4, 0)
    spread_embed(4, 1)
    value_columns(4)
    weigh(4)

    for k in range(1, 5):
        xd = lax.rem(x + k, 4)
        part = dot(evt[xd], at[xd].reshape(2048, 256), ((1,), (0,)))
        if k == 4:
            heads = jnp.where(c == 0, part[:64], part[64:])
        part = part.astype(BF)
        hp[2 * xd] = part[:64]
        hp[2 * xd + 1] = part[64:]
        if k < 4:
            for cd in range(2):
                send(hp.at[2 * xd + cd], hr.at[s], hr_rs.at[s], dev(2 * xd + cd, p))
        else:
            send(hp.at[2 * x + 1 - c], hr.at[s], hr_rs.at[s], partner)
    for sd in line_ids:
        wait(hr.at[sd], hr_rs.at[sd])
        heads = heads + hr[sd].astype(F32)
    hg[s] = heads.astype(BF)
    for sd in line_ids:
        send(hg.at[s], hg.at[s], hg_rs.at[s], dev(sd, p))
    for sd in line_ids:
        wait(hg.at[sd], hg_rs.at[sd])
    for k in range(8):
        wait(ow.at[k], ow_rs.at[k])

    mixed = dot(hg[...].reshape(512, 256), ow[...].reshape(512, 1024), ((0,), (0,)))
    ms[...] = mixed.astype(BF).reshape(16, 16, 1024)
    pltpu.make_async_copy(ms.at[p], mr.at[p], mr_rs.at[0]).start()
    for k in range(1, 16):
        pd = wrap16(p + k)
        send(ms.at[pd], mr.at[p], mr_rs.at[0], dev(s, pd))
    wait(mr, mr_rs.at[0])
    final = mr[0].astype(F32)
    for k in range(1, 16):
        final = final + mr[k].astype(F32)
    for k in range(8):
        ob[k] = final[2 * k : 2 * k + 2, :]
    pltpu.make_async_copy(ob.at[s], out_ref.at[s], ob_rs.at[s]).start()
    for sd in line_ids:
        send(ob.at[sd], out_ref.at[s], ob_rs.at[s], dev(sd, p))
    for k in range(8):
        wait(out_ref.at[k], ob_rs.at[k])

    for ref, sem in pending:
        wait(ref, sem)
    @pl.when(jnp.logical_not(at_home))
    def _():
        drain(across)

    @pl.when(source)
    def _():
        drain(first_sends)


def body(pixels, embed_w, var_embed, key_w, query, value_t, out_w):
    hbm = pl.BlockSpec(memory_space=pl.ANY)
    dma = pltpu.SemaphoreType.DMA
    slices = pl.pallas_call(
        kernel,
        out_shape=jax.ShapeDtypeStruct((8, 2, 1024), F32),
        in_specs=[hbm] * 7,
        out_specs=hbm,
        scratch_shapes=[
            pltpu.VMEM((1, D), F32),
            pltpu.VMEM((16, 256), BF),
            pltpu.VMEM((1, D), BF),
            pltpu.VMEM((64, D), BF),
            pltpu.VMEM((16, D), BF),
            pltpu.VMEM((8, 1, 1024), F32),
            pltpu.VMEM((16, 256), BF),
            pltpu.VMEM((6, 1024, 256), BF),
            pltpu.VMEM((64, 128), BF),
            pltpu.VMEM((16, 64, 128), BF),
            pltpu.VMEM((16, 128, 1024), BF),
            pltpu.VMEM((6, 1, 1024), F32),
            pltpu.VMEM((16, 6, 16, 256), BF),
            pltpu.VMEM((8, 64, 1024), BF),
            pltpu.VMEM((8, 64, 1024), BF),
            pltpu.VMEM((8, 6, 16, 128), F32),
            pltpu.VMEM((8, 6, 16, 128), F32),
            pltpu.VMEM((16, 8, 128), F32),
            pltpu.VMEM((16, 8, 128), F32),
            pltpu.VMEM((8, 16, 8, 128), BF),
            pltpu.VMEM((4, 128, 2048), BF),
            pltpu.VMEM((4, 16, 128, 256), BF),
            pltpu.VMEM((8, 64, 256), BF),
            pltpu.VMEM((8, 64, 256), BF),
            pltpu.VMEM((8, 64, 256), BF),
            pltpu.VMEM((16, 16, 1024), BF),
            pltpu.VMEM((16, 16, 1024), BF),
            pltpu.VMEM((8, 2, 1024), F32),
            dma((5,)),
            dma((1,)),
            dma((6,)),
            dma((6,)),
            dma((6,)),
            dma((1,)),
            dma((8,)),
            dma((8,)),
            dma((2, 16)),
            dma((2, 16)),
            dma((2, 16)),
            dma((8,)),
            dma((1,)),
            dma((8,)),
            dma((8,)),
            dma((8,)),
            dma((1,)),
            dma((8,)),
        ],
        compiler_params=pltpu.CompilerParams(collective_id=0, has_side_effects=True, vmem_limit_bytes=56 * 1024 * 1024),
    )(pixels.transpose(0, 2, 1), embed_w, var_embed, key_w, query.reshape(1, D), value_t, out_w)
    return slices.transpose(1, 0, 2).reshape(2, D).astype(BF)


def solution(mesh):
    placed = (
        P("dev", None, None),
        P("dev", None, None),
        P("dev", None),
        P("dev", None),
        P(),
        P("dev", None),
        P("dev", None),
    )
    return jax.shard_map(body, mesh=mesh, in_specs=placed, out_specs=P("dev", None), check_vma=False)
```

time: 87.8 us -> 76.4 us (0.87)
  Pallas kernels: 86.1 us -> 74.7 us
    pallas_call x1, Pallas kernels: 86.1 us -> 74.7 us  [body(): pl.pallas_call(kernel, out_shape=jax.ShapeDtypeStruct((8, 2, 1024), F32),...]
where the time goes in v3:
time: 76.4 us; the launch traced here: 76.2 us
  Pallas kernels  74.7 us (98%)
  other arithmetic  1.48 us (2%)
    pallas_call x1, Pallas kernels, body(): pl.pallas_call(kernel, out_shape=jax.ShapeDtypeStruct((8, 2, 1024), F32),...  74.7 us

profile of v3, /device:TPU:1, one launch (start us, length us, event | category | flops | bytes accessed | tf_op | source)
XLA Modules:
  0.0 76.2 jit_solution(9793255210261244627)
XLA Ops:
  0.0 74.7 %shard_map.73 = f32[8,2,1024]{2,1,0:T(2,128)} custom-call(bf16[1,16,256]{2,1,0:T(8,128)(2,1)} %bitcast.6, bf16[1,16,8192]{2,1,0:T(8,128)(2,1)} %ew_ref.1, bf16[1,8192]{1,0:T(2,128)(2,1)} %var_ref.1, bf16[64,8192]{1,0:T(8,128)(2,1)} %kw_ref.1, f32[1,8192]{1,0:T(1,128)} %bitcast.5, bf16[64,8192]{1,0:T(8,128)(2,1)} %vt_ref.1, bf16[64,8192]{1,0:T(8,128)(2,1)} %ow_ref.1), custom_call_target="tpu_custom_call" | custom-call | tf_op jit(solution)/shard_map/pallas_call | solution.py:424
  74.7 1.5 %convert_element_type.9 = bf16[8,2,1024]{2,1,0:T(2,128)(2,1)} convert(f32[8,2,1024]{2,1,0:T(2,128)} %shard_map.73) | non-fusion elementwise | flops 16384 | bytes 98304 | tf_op jit(solution)/shard_map/convert_element_type | solution.py:479
